TPU v7x, 32 devices: a whole 2x2x4 slice. The times are simulated.
32 devices in a mesh: front: 4 (over x, core), grid: 8 (over z, y).
Axes of the slice: x: 2, y: 2, z: 4, core: 2. Of those that a mesh axis runs over, the one named last changes fastest.
Arguments:
- index_map: int32 [4, 8192], P('front'), may hold values from 0 to 16383, as said below
- lengths: int32 [4], P('front'), may hold values from 1 to 8192, 24576 in all
- update_front: float32 [4, 8192, 8192], P('front', 'grid'), may hold values from -0.0625 to 0.0625
- front_matrix: float32 [16384, 16384], P(('front', 'grid')), may hold values from -0.046875 to 0.046875
- random: float32 [16384, 256], P(('front', 'grid')), may hold values from -6 to 6
Outputs:
- parent_sample: float32 [16384, 256], P(('front', 'grid'))
Inputs may be any that keep to these rules, and one draw needn't show every extreme that they name: `index_map`: within one child the 8192 entries are distinct parent rows. `lengths`: rows of a child at or past its length are not live; the largest length equals 8192.
All inputs are finite; a program needn't handle non-finite values. No bound on the sum of `lengths` on one device may be relied on, other than what follows from the above.
Results may differ from a plain program's by a relative error of at most 0.0003.
Values sent between devices are 32-bit elements; how exact they have to be, the bound alone decides.
A program may use at most 192 MiB of HBM per device.

v0:
```python
import jax
import jax.numpy as jnp
from jax import lax
from jax.sharding import PartitionSpec as P


def shards(index_map, lengths, update_front, front_matrix, random):
    gathered_random = lax.all_gather(random, ("front", "grid"), axis=0, tiled=True)
    parent_part = jnp.dot(
        front_matrix,
        gathered_random,
        preferred_element_type=jnp.float32,
        precision=lax.Precision.HIGHEST,
    )
    index_rows = index_map[0]
    child_random = jnp.take(gathered_random, index_rows, axis=0)
    child_sample = jnp.dot(
        update_front[0],
        child_random,
        preferred_element_type=jnp.float32,
        precision=lax.Precision.HIGHEST,
    )
    local_rows = child_sample.shape[0]
    first_row = lax.axis_index("grid") * local_rows
    row_numbers = first_row + jnp.arange(local_rows, dtype=jnp.int32)
    live_rows = row_numbers < lengths[0]
    child_sample = jnp.where(live_rows[:, None], child_sample, jnp.float32(0.0))
    own_rows = parent_part.shape[0]
    group_sample = lax.all_gather(child_sample, "grid", axis=0, tiled=True)
    group_count = lax.axis_size("front")
    grid_count = lax.axis_size("grid")
    grid_place = lax.axis_index("grid")
    block_ids = jnp.arange(group_count, dtype=jnp.int32)[:, None] * grid_count + grid_place
    targets = (block_ids * own_rows + jnp.arange(own_rows, dtype=jnp.int32)[None, :]).reshape(-1)
    one_hot = (targets[:, None] == index_rows[None, :]).astype(jnp.float32)
    terms = jnp.dot(
        one_hot, group_sample, preferred_element_type=jnp.float32, precision=lax.Precision.HIGHEST
    )
    terms = terms.reshape(group_count, own_rows, terms.shape[1])
    added = lax.psum_scatter(terms, "front", scatter_dimension=0, tiled=True)[0]
    return parent_part + added


def solution(mesh):
    placed = (
        P("front", None),
        P("front"),
        P("front", "grid", None),
        P(("front", "grid"), None),
        P(("front", "grid"), None),
    )
    return jax.shard_map(
        shards, mesh=mesh, in_specs=placed, out_specs=P(("front", "grid"), None), check_vma=False
    )
```

profile of v0, /device:TPU:0, one launch (start us, length us, event | category | flops | bytes accessed | tf_op | source)
XLA Modules:
  0.0 452.4 jit_solution(5761068284359675660)
XLA Ops:
  6.5 0.0 all-gather.3.cloned.1.call-start
  6.5 0.7 all-gather.3.cloned.1.call-update
  7.3 0.0 all-gather.5.cloned.1.call-start
  8.0 0.8 compare_and_fusion
  8.7 0.8 compare_select_fusion
  9.6 118.0 %all-gather.3.cloned.1.call-done = f32[16384,256]{1,0:T(8,128)} async-done(((f32[512,256]{1,0:T(8,128)}), f32[16384,256]{1,0:T(8,128)}) %all-gather.3.cloned.1.call-update) | async-done | bytes 16777232 | tf_op jit(solution)/shard_map/all_gather | solution.py:8
  127.5 37.1 %gather_fusion = f32[8192,256]{1,0:T(8,128)} fusion(f32[16384,256]{1,0:T(8,128)} %all-gather.3.cloned.1.call-done, s32[8192]{0:T(1024)S(1)} %broadcast_clamp_fusion), kind=kCustom, calls=%fused_computation | custom fusion | bytes 16809984 | tf_op jit(solution)/shard_map/jit(_take)/gather | solution.py:16
  164.7 0.0 copy-start
  164.7 59.7 %fusion.14 = f32[1024,256]{0,1:T(8,128)} fusion(f32[1,1024,8192]{2,1,0:T(8,128)} %param.7, f32[8192,256]{1,0:T(8,128)} %gather_fusion, pred[8192]{0:T(1024)(128)(4,1)S(1)} %compare_and_fusion, pred[1024]{0:T(1024)(128)(4,1)S(1)} %add_compare_fusion), kind=kOutput, calls=%fused_computation.11 | convolution fusion | flops 25772163072 | bytes 43000832 | tf_op jit(solution)/shard_map/dot_general | solution.py:17
  224.3 0.0 all-gather.5.cloned.1.call-update
  224.3 0.2 reduce-scatter.2.cloned.1.call-start
  224.6 0.1 add_bitcast_fusion
  224.7 122.5 %all-gather.5.cloned.1.call-done = f32[8192,256]{0,1:T(8,128)} async-done(((f32[1024,256]{0,1:T(8,128)}), f32[8192,256]{0,1:T(8,128)}) %all-gather.5.cloned.1.call-update) | async-done | bytes 8388624 | tf_op jit(solution)/shard_map/all_gather | solution.py:29
  347.2 0.0 copy-done
  347.2 36.9 %fusion = f32[2048,256]{1,0:T(8,128)} fusion(f32[8192,256]{0,1:T(8,128)} %all-gather.5.cloned.1.call-done, s32[8192]{0:T(1024)S(1)} %bitcast.26, s32[2048]{0:T(1024)S(1)} %bitcast.28), kind=kOutput, calls=%fused_computation.1 | convolution fusion | flops 51556384768 | bytes 10526720 | tf_op jit(solution)/shard_map/dot_general | solution.py:36
  384.1 0.0 reduce-scatter.2.cloned.1.call-update
  384.1 29.5 %reduce-scatter.2.cloned.1.call-done = f32[1,512,256]{2,1,0:T(8,128)} async-done(((f32[4,512,256]{2,1,0:T(8,128)}), f32[1,512,256]{2,1,0:T(8,128)}) %reduce-scatter.2.cloned.1.call-update) | async-done | bytes 524304 | tf_op jit(solution)/shard_map/reduce_scatter | solution.py:40
  413.6 32.3 %convolution_add_fusion = f32[512,256]{1,0:T(8,128)} fusion(f32[512,16384]{1,0:T(8,128)} %param.8, f32[16384,256]{1,0:T(8,128)} %all-gather.3.cloned.1.call-done, f32[1,512,256]{2,1,0:T(8,128)} %reduce-scatter.2.cloned.1.call-done), kind=kOutput, calls=%fused_computation.12 | convolution fusion | flops 25769934848 | bytes 51380224 | tf_op jit(solution)/shard_map/dot_general | solution.py:9
  (4 shorter events, 0.0 us)
Async XLA Ops:
  6.5 121.0 %all-gather.3.cloned.1.call-start = ((), (), s32[]{:S(2)}) async-start(), calls=%async_computation.1 | async-start | bytes 17301504 | tf_op jit(solution)/shard_map/all_gather | solution.py:8
  7.3 339.9 %all-gather.5.cloned.1.call-start = ((), (), s32[]{:S(2)}) async-start(), calls=%async_computation.2 | async-start | bytes 9437184 | tf_op jit(solution)/shard_map/all_gather | solution.py:29
  164.7 182.5 %copy-start = (s32[1,8192]{1,0:T(1,128)S(1)}, s32[1,8192]{1,0:T(1,128)}, u32[]{:S(2)}) copy-start(s32[1,8192]{1,0:T(1,128)} %param.5) | copy-start | bytes 98308
  224.3 189.2 %reduce-scatter.2.cloned.1.call-start = ((), (), s32[]{:S(2)}) async-start(), calls=%async_computation.3 | async-start | bytes 2621440 | tf_op jit(solution)/shard_map/reduce_scatter | solution.py:40
Sparse Core Ops, SparseCore 0:
  10.4 117.0 all-gather.2
  224.5 122.6 all-gather.4
  384.2 29.3 reduce-scatter.1
where the time goes:
time: 453 us; the launch traced here: 452 us
  waiting for transfers between devices  271 us (60%)
  matrix products  129 us (28%)
  local copies, waits for them, and re-layouts  37.2 us (8%)
  between operations  13.8 us (3%)
    all_gather x1, waiting for transfers between devices, shards(): group_sample = lax.all_gather(child_sample, 'grid', axis=0, tiled=True)  123 us
    all_gather x1, waiting for transfers between devices, shards(): lax.all_gather(random, ('front', 'grid'), axis=0, tiled=True)  118 us
    dot_general x1, matrix products, shards(): jnp.dot(update_front[0], child_random, preferred_element_type=jnp.float32...  59.7 us
    gather x1, local copies, waits for them, and re-layouts, shards(): child_random = jnp.take(gathered_random, index_rows, axis=0)  37.1 us
    dot_general x1, matrix products, shards(): jnp.dot(one_hot, group_sample, preferred_element_type=jnp.float32, precis...  36.9 us
    dot_general x1, matrix products, shards(): jnp.dot(front_matrix, gathered_random, preferred_element_type=jnp.float32...  32.3 us
    reduce_scatter x1, waiting for transfers between devices, shards(): added = lax.psum_scatter(terms, 'front', scatter_dimension=0, tiled=True)[0]  29.5 us
  transfers between devices with their start and end apart: 3, of which 3 were waited for; matrix products, arithmetic and copies ran while one was open for 0% of the time, Pallas kernels for 0%

commit v1 on v0

--- a/solution.py
+++ b/solution.py
@@ -26,7 +26,9 @@
     live_rows = row_numbers < lengths[0]
     child_sample = jnp.where(live_rows[:, None], child_sample, jnp.float32(0.0))
     own_rows = parent_part.shape[0]
-    group_sample = lax.all_gather(child_sample, "grid", axis=0, tiled=True)
+    group_sample = jnp.concatenate(
+        lax.all_to_all(jnp.stack([child_sample] * lax.axis_size("grid")), "grid", 0, 0), axis=0
+    )
     group_count = lax.axis_size("front")
     grid_count = lax.axis_size("grid")
     grid_place = lax.axis_index("grid")

time: 453 us -> 525 us (1.16)
  waiting for transfers between devices: 271 us -> 332 us
    all_to_all x0 -> x1, waiting for transfers between devices: none -> 183 us  [shards(): lax.all_to_all(jnp.stack([child_sample] * lax.axis_size('grid')), 'grid',...]
    all_gather x1 -> x0, waiting for transfers between devices: 123 us -> none  [shards(): group_sample = lax.all_gather(child_sample, 'grid', axis=0, tiled=True)]
where the time goes in v1:
time: 525 us
  waiting for transfers between devices  332 us (63%)
  matrix products  130 us (25%)
  local copies, waits for them, and re-layouts  41.6 us (8%)
  between operations  14.1 us (3%)
    all_to_all x1, waiting for transfers between devices, shards(): lax.all_to_all(jnp.stack([child_sample] * lax.axis_size('grid')), 'grid',...  183 us
    all_gather x1, waiting for transfers between devices, shards(): lax.all_gather(random, ('front', 'grid'), axis=0, tiled=True)  118 us
    dot_general x1, matrix products, shards(): jnp.dot(update_front[0], child_random, preferred_element_type=jnp.float32...  58.6 us
    dot_general x1, matrix products, shards(): jnp.dot(one_hot, group_sample, preferred_element_type=jnp.float32, precis...  39 us
    gather x1, local copies, waits for them, and re-layouts, shards(): child_random = jnp.take(gathered_random, index_rows, axis=0)  37.3 us
    dot_general x1, matrix products, shards(): jnp.dot(front_matrix, gathered_random, preferred_element_type=jnp.float32...  32.3 us
    reduce_scatter x1, waiting for transfers between devices, shards(): added = lax.psum_scatter(terms, 'front', scatter_dimension=0, tiled=True)[0]  30.1 us
  transfers between devices with their start and end apart: 3, of which 3 were waited for; matrix products, arithmetic and copies ran while one was open for 0% of the time, Pallas kernels for 0%

profile of v1, /device:TPU:0, one launch (start us, length us, event | category | flops | bytes accessed | tf_op | source)
XLA Modules:
  0.0 524.8 jit_solution(2086127214786789393)
XLA Ops:
  6.5 0.0 all-gather.2.cloned.1.call-start
  6.5 0.7 all-gather.2.cloned.1.call-update
  7.9 0.8 compare_and_fusion
  8.7 0.8 compare_select_fusion
  9.5 118.0 %all-gather.2.cloned.1.call-done = f32[16384,256]{1,0:T(8,128)} async-done(((f32[512,256]{1,0:T(8,128)}), f32[16384,256]{1,0:T(8,128)}) %all-gather.2.cloned.1.call-update) | async-done | bytes 16777232 | tf_op jit(solution)/shard_map/all_gather | solution.py:8
  127.5 37.3 %gather_fusion = f32[8192,256]{1,0:T(8,128)} fusion(f32[16384,256]{1,0:T(8,128)} %all-gather.2.cloned.1.call-done, s32[8192]{0:T(1024)S(1)} %broadcast_clamp_fusion), kind=kCustom, calls=%fused_computation | custom fusion | bytes 16809984 | tf_op jit(solution)/shard_map/jit(_take)/gather | solution.py:16
  164.8 58.6 %fusion.14 = f32[1024,256]{0,1:T(8,128)S(1)} fusion(f32[1,1024,8192]{2,1,0:T(8,128)} %param.7, f32[8192,256]{1,0:T(8,128)} %gather_fusion, pred[8192]{0:T(1024)(128)(4,1)S(1)} %compare_and_fusion, pred[1024]{0:T(1024)(128)(4,1)S(1)} %add_compare_fusion), kind=kOutput, calls=%fused_computation.11 | convolution fusion | flops 25772163072 | bytes 43000832 | tf_op jit(solution)/shard_map/dot_general | solution.py:17
  223.4 0.0 copy-start
  223.4 0.3 copy.7
  223.8 3.9 stack.2
  227.7 5.0 all-to-all-start
  232.7 0.2 reduce-scatter.2.cloned.1.call-start
  232.9 0.1 iota_add_fusion
  233.0 183.4 %all-to-all-done = f32[8,1024,256]{2,1,0:T(8,128)} async-done(((f32[8,1024,256]{2,1,0:T(8,128)}), f32[8,1024,256]{2,1,0:T(8,128)}, u32[]{:S(2)}, u32[]{:S(2)}) %all-to-all-start) | async-done | bytes 8388640 | tf_op jit(solution)/shard_map/all_to_all | solution.py:30
  416.4 0.0 copy-done
  416.4 39.0 %fusion = f32[4,512,256]{2,1,0:T(8,128)} fusion(f32[8192,256,1]{1,0,2:T(8,128)} %bitcast.7, s32[8192]{0:T(1024)S(1)} %bitcast.24, s32[4,512]{1,0:T(4,128)S(1)} %iota_add_fusion), kind=kOutput, calls=%fused_computation.1 | convolution fusion | flops 51556384768 | bytes 10526720 | tf_op jit(solution)/shard_map/dot_general | solution.py:38
  455.5 0.0 reduce-scatter.2.cloned.1.call-update
  455.5 30.1 %reduce-scatter.2.cloned.1.call-done = f32[1,512,256]{2,1,0:T(8,128)} async-done(((f32[4,512,256]{2,1,0:T(8,128)}), f32[1,512,256]{2,1,0:T(8,128)}) %reduce-scatter.2.cloned.1.call-update) | async-done | bytes 524304 | tf_op jit(solution)/shard_map/reduce_scatter | solution.py:42
  485.6 32.3 %convolution_add_fusion = f32[512,256]{1,0:T(8,128)} fusion(f32[512,16384]{1,0:T(8,128)} %param.8, f32[16384,256]{1,0:T(8,128)} %all-gather.2.cloned.1.call-done, f32[1,512,256]{2,1,0:T(8,128)} %reduce-scatter.2.cloned.1.call-done), kind=kOutput, calls=%fused_computation.12 | convolution fusion | flops 25769934848 | bytes 51380224 | tf_op jit(solution)/shard_map/dot_general | solution.py:9
  (3 shorter events, 0.0 us)
Async XLA Ops:
  6.5 121.0 %all-gather.2.cloned.1.call-start = ((), (), s32[]{:S(2)}) async-start(), calls=%async_computation.2 | async-start | bytes 17301504 | tf_op jit(solution)/shard_map/all_gather | solution.py:8
  223.4 193.0 %copy-start = (s32[1,8192]{1,0:T(1,128)S(1)}, s32[1,8192]{1,0:T(1,128)}, u32[]{:S(2)}) copy-start(s32[1,8192]{1,0:T(1,128)} %param.5) | copy-start | bytes 98308
  227.7 188.7 %all-to-all-start = ((f32[8,1024,256]{2,1,0:T(8,128)}), f32[8,1024,256]{2,1,0:T(8,128)}, u32[]{:S(2)}, u32[]{:S(2)}) async-start(f32[8,1024,256]{2,1,0:T(8,128)} %stack.2), calls=%async_computation | async-start | bytes 16777216 | tf_op jit(solution)/shard_map/all_to_all | solution.py:30
  232.7 252.9 %reduce-scatter.2.cloned.1.call-start = ((), (), s32[]{:S(2)}) async-start(), calls=%async_computation.3 | async-start | bytes 2621440 | tf_op jit(solution)/shard_map/reduce_scatter | solution.py:42
Sparse Core Ops, SparseCore 0:
  10.4 117.0 all-gather.1
  455.6 29.9 reduce-scatter.1
